TPU v7x, 32 devices: a whole 2x2x4 slice. The times are simulated.
32 devices in a mesh: row: 4 (over y, core), col: 8 (over z, x).
Axes of the slice: x: 2, y: 2, z: 4, core: 2. Of those that a mesh axis runs over, the one named last changes fastest.
Arguments:
- fluid_data: float32 [51, 8192], P(None, ('row', 'col')), as said below
- center_data: float32 [51, 8192], P(None, ('col', 'row')), as said below
- poly_coef: float32 [48, 4], replicated, may hold values from -3 to 3
Outputs:
- fluid_motion: float32 [48, 8192], P(None, ('row', 'col'))
- center_load: float32 [48, 8192], P(None, ('col', 'row'))
Inputs may be any that keep to these rules, and one draw needn't show every extreme that they name: Rows 0 to 2 of fluid_data lie in [0, 1]; rows 3 and on are forces. Rows 0 and 1 of center_data lie in [0, 1] and row 2 lies in [-0.5, -0.02], so every center is at least 0.02 below every vertex; rows 3 and on are coefficients.
All inputs are finite; a program needn't handle non-finite values.
Results may differ from a plain program's by a relative error of at most 0.0003.
Values sent between devices are 32-bit elements; how exact they have to be, the bound alone decides.
A program may use at most 64 MiB of HBM per device.

v0:
```python
import functools

import jax
import jax.numpy as jnp
from jax import lax
from jax.experimental import pallas as pl
from jax.experimental.pallas import tpu as pltpu
from jax.sharding import PartitionSpec as P

WAVES = 64
MESH = pl.DeviceIdType.MESH
TOP = 12.404427306735432
MID = 0.6418441597071612
LOW = 0.16126480593510223


def paired(me, m, n):
    other, bit = 0, 1
    while bit < n:
        other = other + (((me // bit) % 2 + (m // bit) % 2) % 2) * bit
        bit *= 2
    return other


def dot(a, b, dims):
    return lax.dot_general(a, b, (dims, ((), ())), preferred_element_type=jnp.float32)


def split(x):
    high = x.astype(jnp.bfloat16)
    low = (x - high.astype(jnp.float32)).astype(jnp.bfloat16)
    return high, low


def body(rows, cols, side, fluid, center, poly, motion, loads, *scratch):
    fl, ce, pv, cp, chl, fhl, kh, kl, mo_out, mo_in, ld_out, ld_in, pre = scratch[:13]
    own, fs, fr, cs, cr, ms, mr, ls, lr, ps, pr = scratch[13:]
    S, T = cols // side, rows * side
    half = T // 2
    row, col = lax.axis_index("row"), lax.axis_index("col")
    my_s, my_t = col // side, (row % 2) * half + (col % side) * (rows // 2) + row // 2
    nvals = pv.shape[1]
    wf, wc = fluid.shape[1], center.shape[1]
    lanes = 128 if wf % 128 == 0 else wf
    step_rows = 32 if wc % 32 == 0 else wc

    def along_s(m):
        return {"row": row, "col": paired(my_s, m, S) * side + col % side}

    def along_t(m):
        i = paired(my_t, m, T)
        return {
            "row": (i % (rows // 2)) * 2 + i // half,
            "col": (col // side) * side + (i % half) // (rows // 2),
        }

    def copy(src, dst, send, recv, where):
        return pltpu.make_async_remote_copy(
            src_ref=src, dst_ref=dst, send_sem=send, recv_sem=recv, device_id=where, device_id_type=MESH
        )

    def send_fluid(m):
        return copy(fl.at[0], fl.at[m], fs.at[m], fr.at[m], along_s(m))

    def send_center(p):
        return copy(ce.at[0], ce.at[p], cs.at[p], cr.at[p], along_t(half if p == 1 else p - 1))

    def hand_on(p):
        q = p + half - 1
        return copy(ce.at[p], ce.at[q], cs.at[q], cr.at[q], along_t(half))

    def send_motion(m):
        return copy(mo_out.at[m], mo_in.at[m], ms.at[m], mr.at[m], along_s(m))

    def send_pre(p):
        j = p - half
        return copy(ld_out.at[p], pre.at[j], ps.at[j], pr.at[j], along_t(half))

    def send_loads(j):
        return copy(ld_out.at[j + 1], ld_in.at[j], ls.at[j], lr.at[j], along_t(j))

    def send_other():
        return copy(ld_out.at[1], ld_in.at[0], ls.at[0], lr.at[0], along_t(half))

    local = [
        pltpu.make_async_copy(center, ce.at[0], own.at[0]),
        pltpu.make_async_copy(fluid, fl.at[0], own.at[1]),
        pltpu.make_async_copy(poly, pv, own.at[2]),
    ]
    for c in local:
        c.start()
    barrier = pltpu.get_barrier_semaphore()
    for p in range(1, half + 1):
        pl.semaphore_signal(barrier, inc=1, device_id=along_t(p), device_id_type=MESH)
    for m in range(1, S):
        pl.semaphore_signal(barrier, inc=1, device_id=along_s(m), device_id_type=MESH)
    for c in local:
        c.wait()
    order_s = [1] + list(range(S - 1, 1, -1))
    pl.semaphore_wait(barrier, S - 1 + half)
    for p in range(1, half + 1):
        send_center(p).start()
    for m in order_s:
        send_fluid(m).start()

    def ready_center(r):
        places = jnp.transpose(ce[r, 0:8, :] * float(WAVES))
        for a in range(3):
            cp[r, a] = jnp.broadcast_to(places[:, a : a + 1], (wc, lanes))
        high, low = split(ce[r, 3:, :] * TOP)
        chl[r, 0:nvals] = high
        chl[r, nvals:] = low
        ld_out[r] = jnp.zeros((nvals, wc), jnp.float32)

    def ready_fluid(m):
        high, low = split(fl[m, 3:, :] * TOP)
        fhl[m, 0:nvals] = high
        fhl[m, nvals:] = low
        mo_out[m] = jnp.zeros((nvals, wf), jnp.float32)

    def values(m, r, slot):
        for h in range(wf // lanes):
            part = pl.ds(h * lanes, lanes)
            fx, fy, fz = (fl[m, a : a + 1, part] * float(WAVES) for a in range(3))
            for j in range(0, wc, step_rows):
                at = pl.ds(j, step_rows)
                dx, dy, dz = cp[r, 0, at, :] - fx, cp[r, 1, at, :] - fy, cp[r, 2, at, :] - fz
                sq = dx * dx + dy * dy + dz * dz
                inv = lax.rsqrt(sq)
                turns = sq * inv
                f = turns - jnp.round(turns)
                size = jnp.abs(f)
                rest = 0.5 - size
                q = size * rest
                value = (f * rest * inv) * ((q + MID) * q + LOW)
                high, low = split(value)
                kh[slot, at, part] = high
                kl[slot, at, part] = low

    def sums(m, r, slot):
        k_high, k_low = kh[slot], kl[slot]
        across = ((1,), (0,))
        wide = dot(chl[r], k_high, across)
        mo_out[m] += wide[:nvals] + wide[nvals:] + dot(chl[r, 0:nvals], k_low, across)
        back = ((1,), (1,))
        wide = dot(fhl[m], k_high, back)
        ld_out[r] += wide[:nvals] + wide[nvals:] + dot(fhl[m, 0:nvals], k_low, back)

    def pair(before, one, two):
        sums(*before, 1)
        values(*one, 0)
        sums(*one, 0)
        values(*two, 1)
        return two

    kh[1] = jnp.zeros((wc, wf), jnp.bfloat16)
    kl[1] = jnp.zeros((wc, wf), jnp.bfloat16)
    ready_fluid(0)
    before = (0, 0)

    for k in range(half):
        for p in (2 * k, 2 * k + 1):
            if 2 <= p <= half:
                send_center(p).wait_recv()
                hand_on(p).start()
            elif p == 1:
                send_center(p).wait_recv()
            elif p > half:
                hand_on(p - half + 1).wait_recv()
            ready_center(p)
        if k == 0:
            send_fluid(order_s[0]).wait_recv()
            ready_fluid(order_s[0])
        m = order_s[0]
        before = pair(before, (m, 2 * k), (m, 2 * k + 1))

    def middle(s, _):
        m = S - s
        send_fluid(m).wait_recv()
        ready_fluid(m)
        last_m = (m + 1) % S + (m + 1) // S

        pair((last_m, T - 1), (m, 0), (m, 1))
        send_motion(last_m).start()

        def inner(k, _):
            pair((m, 2 * k - 1), (m, 2 * k), (m, 2 * k + 1))
            return 0

        lax.fori_loop(1, half, inner, 0)
        return 0

    lax.fori_loop(1, S - 2, middle, 0)

    far = order_s[-1]
    prior = order_s[-2]
    send_fluid(far).wait_recv()
    ready_fluid(far)
    pair((prior, T - 1), (far, T - 1), (0, T - 1))
    send_motion(prior).start()

    def mixed(k, _):
        r = T - 1 - k
        pair((0, r + 1), (far, r), (0, r))
        send_pre(r + 1).start()
        return 0

    lax.fori_loop(1, half, mixed, 0)

    def finish(j):
        send_pre(half + j).wait_recv()
        ld_out[j + 1] += pre[j]
        send_loads(j).start()

    pair((0, half), (far, half - 1), (far, half - 2))
    finish(half - 1)

    def far_rest(k, _):
        r = half - 1 - 2 * k
        pair((far, r + 1), (far, r), (far, r - 1))
        return 0

    lax.fori_loop(1, half // 2, far_rest, 0)
    pair((far, 0), (0, half - 1), (0, half - 2))
    send_motion(far).start()
    finish(half - 2)

    def own_rest(k, _):
        r = half - 1 - 2 * k
        pair((0, r + 1), (0, r), (0, r - 1))
        finish(r)

        @pl.when(r > 1)
        def _():
            finish(r - 1)

        return 0

    lax.fori_loop(1, half // 2, own_rest, 0)
    send_other().start()
    sums(0, 0, 1)

    total = mo_out[0]
    affine = jnp.transpose(pv[...])
    for a in range(3):
        total = total + affine[:, a + 1 : a + 2] * fl[0, a : a + 1, :]
    total = total + affine[:, 0:1]
    for m in order_s:
        send_motion(m).wait_recv()
        total = total + mo_in[m]
    motion[...] = total
    total = ld_out[0]
    for j in range(half - 1, 0, -1):
        send_loads(j).wait_recv()
        total = total + ld_in[j]
    send_other().wait_recv()
    loads[...] = total + ld_in[0]
    for m in order_s:
        send_fluid(m).wait_send()
        send_motion(m).wait_send()
    for p in range(1, half + 1):
        send_center(p).wait_send()
    for p in range(2, half + 1):
        hand_on(p).wait_send()
        send_pre(p + half - 1).wait_send()
        send_loads(p - 1).wait_send()
    send_other().wait_send()


def per_device(rows, cols, side, fluid_data, center_data, poly_coef):
    f32, bf16 = jnp.float32, jnp.bfloat16
    S, T = cols // side, rows * side
    height, wf = fluid_data.shape
    wc = center_data.shape[1]
    n = height - 3
    lanes = 128 if wf % 128 == 0 else wf
    vmem = pl.BlockSpec(memory_space=pltpu.VMEM)
    hbm = pl.BlockSpec(memory_space=pltpu.HBM)
    sems = [pltpu.SemaphoreType.DMA((k,)) for k in (3, S, S, T, T, S, S, T // 2, T // 2, T // 2, T // 2)]
    return pl.pallas_call(
        functools.partial(body, rows, cols, side),
        out_shape=(jax.ShapeDtypeStruct((n, wf), f32), jax.ShapeDtypeStruct((n, wc), f32)),
        in_specs=[hbm] * 3,
        out_specs=(vmem, vmem),
        scratch_shapes=[
            pltpu.VMEM((S, height, wf), f32),
            pltpu.VMEM((T, height, wc), f32),
            pltpu.VMEM((4, n), f32),
            pltpu.VMEM((T, 3, wc, lanes), f32),
            pltpu.VMEM((T, 2 * n, wc), bf16),
            pltpu.VMEM((S, 2 * n, wf), bf16),
            pltpu.VMEM((2, wc, wf), bf16),
            pltpu.VMEM((2, wc, wf), bf16),
            pltpu.VMEM((S, n, wf), f32),
            pltpu.VMEM((S, n, wf), f32),
            pltpu.VMEM((T, n, wc), f32),
            pltpu.VMEM((T // 2, n, wc), f32),
            pltpu.VMEM((T // 2, n, wc), f32),
            *sems,
        ],
        compiler_params=pltpu.CompilerParams(
            collective_id=0, has_side_effects=True, vmem_limit_bytes=67_043_328
        ),
    )(fluid_data, center_data, poly_coef.T)


def solution(mesh):
    rows, cols = mesh.shape["row"], mesh.shape["col"]
    side = 2 if cols % 2 == 0 else 1
    placed = (P(None, ("row", "col")), P(None, ("col", "row")), P())
    return jax.shard_map(
        functools.partial(per_device, rows, cols, side),
        mesh=mesh,
        in_specs=placed,
        out_specs=(P(None, ("row", "col")), P(None, ("col", "row"))),
        check_vma=False,
    )
```

profile of v0, /device:TPU:0, one launch (start us, length us, event | category | flops | bytes accessed | tf_op | source)
XLA Modules:
  0.0 28.9 jit_solution(3525524753247699579)
XLA Ops:
  0.6 26.2 %shard_map.50 = (f32[48,256]{1,0:T(8,128)}, f32[48,256]{1,0:T(8,128)}) custom-call(f32[51,256]{1,0:T(8,128)} %fluid.1, f32[51,256]{1,0:T(8,128)} %center.1, f32[4,48]{1,0:T(4,128)} %bitcast.1), custom_call_target="tpu_custom_call" | custom-call | tf_op jit(solution)/shard_map/pallas_call | solution.py:280
  26.8 0.0 copy-start
  26.8 1.4 %copy.7 = f32[48,256]{1,0:T(8,128)} copy(f32[48,256]{1,0:T(8,128)} %get-tuple-element.4) | data formatting | bytes 98304
  28.3 0.0 copy-done
  28.3 0.6 %copy.8 = f32[48,256]{1,0:T(8,128)} copy(f32[48,256]{1,0:T(8,128)S(1)} %copy-done) | data formatting | bytes 98304
Async XLA Ops:
  26.8 1.4 %copy-start = (f32[48,256]{1,0:T(8,128)S(1)}, f32[48,256]{1,0:T(8,128)}, u32[]{:S(2)}) copy-start(f32[48,256]{1,0:T(8,128)} %get-tuple-element.5) | copy-start | bytes 147460
where the time goes:
time: 29.1 us; the launch traced here: 28.9 us
  Pallas kernels  26.2 us (90%)
  local copies, waits for them, and re-layouts  2.06 us (7%)
  between operations  0.65 us (2%)
    pallas_call x1, Pallas kernels, per_device(): pl.pallas_call(functools.partial(body, rows, cols, side), out_shape=(jax....  26.2 us
    unnamed x4, local copies, waits for them, and re-layouts  2.06 us

commit v1 on v0

v1 whole, which is shorter than its diff:
```python
import functools

import jax
import jax.numpy as jnp
from jax import lax
from jax.experimental import pallas as pl
from jax.experimental.pallas import tpu as pltpu
from jax.sharding import PartitionSpec as P

WAVES = 64
MESH = pl.DeviceIdType.MESH
TOP = 12.404427306735432
MID = 0.6418441597071612
LOW = 0.16126480593510223
DEPTH = 128


def paired(me, m, n):
    other, bit = 0, 1
    while bit < n:
        other = other + (((me // bit) % 2 + (m // bit) % 2) % 2) * bit
        bit *= 2
    return other


def dot(a, b, dims):
    return lax.dot_general(a, b, (dims, ((), ())), preferred_element_type=jnp.float32)


def rounded(x):
    return x.astype(jnp.bfloat16).astype(jnp.float32)


def split(x):
    high = x.astype(jnp.bfloat16)
    low = (x - high.astype(jnp.float32)).astype(jnp.bfloat16)
    return high, low


def pieces(places):
    x = places * float(WAVES)
    coarse = jnp.round(x * 2.0) * 0.5
    fine = x - coarse
    coarse = coarse - float(WAVES // 2)
    first = rounded(fine)
    second = rounded(fine - first)
    fine = first + second
    large = coarse * coarse
    small = fine * (coarse + coarse) + fine * fine
    large = large[0:1] + large[1:2] + large[2:3]
    small = small[0:1] + small[1:2] + small[2:3]
    l1 = rounded(large)
    l2 = large - l1
    s1 = rounded(small)
    s2 = rounded(small - s1)
    s3 = small - s1 - s2
    return coarse, first, second, (l1, l2), (s1, s2, s3)


def rows_of(base, at, extra):
    out = jnp.where(at < 3, base, 0.0)
    for i, e in extra:
        out = jnp.where(at == i, e, out)
    return out


def center_rows(places):
    c, f1, f2, large, small = pieces(places)
    at = lax.broadcasted_iota(jnp.int32, places.shape, 0)
    one = 1.0
    return [
        rows_of(c, at, [(3, large[0]), (4, large[1]), (5, one), (6, one)]),
        rows_of(c, at, [(3, small[0]), (4, small[1]), (5, small[2])]),
        rows_of(c, at, [(3, one), (4, one), (5, one)]),
        rows_of(f1, at, []),
        rows_of(f2, at, []),
        rows_of(f1, at, []),
        rows_of(f1, at, []),
        rows_of(f2, at, []),
        rows_of(f2, at, []),
    ]


def fluid_rows(places):
    c, f1, f2, large, small = pieces(places)
    at = lax.broadcasted_iota(jnp.int32, places.shape, 0)
    one = 1.0
    c, f1, f2 = -2.0 * c, -2.0 * f1, -2.0 * f2
    return [
        rows_of(c, at, [(3, one), (4, one), (5, large[0]), (6, large[1])]),
        rows_of(f1, at, [(3, one), (4, one), (5, one)]),
        rows_of(f2, at, [(3, small[0]), (4, small[1]), (5, small[2])]),
        rows_of(c, at, []),
        rows_of(c, at, []),
        rows_of(f1, at, []),
        rows_of(f2, at, []),
        rows_of(f1, at, []),
        rows_of(f2, at, []),
    ]


def tiles_of(S, T):
    half = T // 2
    near = list(range(1, min(half, 3)))
    order = [(0, 0), (0, half)]
    order += [(0, p) for p in near] + [(1, p) for p in near]
    for p in near:
        order += [(0, half + p), (1, half + p)]
    for p in range(3, half):
        order += [(0, p), (1, p), (0, half + p), (1, half + p)]
    for m in range(S - 1, 2, -1):
        order += [(m, r) for r in [0, half] + list(range(1, half)) + list(range(half + 1, T))]
    order += [(2, r) for r in list(range(T - 1, half, -1)) + list(range(half - 1, 0, -1)) + [half, 0]]
    order += [(1, 0), (1, half)]
    assert len(set(order)) == S * T == len(order)
    return order


def body(rows, cols, side, fluid, center, poly, motion, loads, *scratch):
    (fl, ce, pv, fa, ff, fc, chl, fhl, sq, kh, kl, mo_out, mo_in, ld_out, ld_in, pre) = scratch[:16]
    own, fs, fr, cs, cr, ms, mr, ls, lr, ps, pr = scratch[16:]
    S, T = cols // side, rows * side
    half = T // 2
    row, col = lax.axis_index("row"), lax.axis_index("col")
    my_s, my_t = col // side, (row % 2) * half + (col % side) * (rows // 2) + row // 2
    nvals = pv.shape[1]
    wf, wc = fluid.shape[1], center.shape[1]

    def along_s(m):
        return {"row": row, "col": paired(my_s, m, S) * side + col % side}

    def along_t(m):
        i = paired(my_t, m, T)
        return {
            "row": (i % (rows // 2)) * 2 + i // half,
            "col": (col // side) * side + (i % half) // (rows // 2),
        }

    def copy(src, dst, send, recv, where):
        return pltpu.make_async_remote_copy(
            src_ref=src, dst_ref=dst, send_sem=send, recv_sem=recv, device_id=where, device_id_type=MESH
        )

    def send_fluid(m):
        return copy(fl.at[0], fl.at[m], fs.at[m], fr.at[m], along_s(m))

    def send_center(p):
        return copy(ce.at[0], ce.at[p], cs.at[p], cr.at[p], along_t(p))

    def hand_on(p):
        q = p + half
        return copy(ce.at[p], ce.at[q], cs.at[q], cr.at[q], along_t(half))

    def send_motion(m):
        return copy(mo_out.at[m], mo_in.at[m], ms.at[m], mr.at[m], along_s(m))

    def send_pre(p):
        j = p - half
        return copy(ld_out.at[p], pre.at[j], ps.at[j], pr.at[j], along_t(half))

    def send_loads(j):
        return copy(ld_out.at[j], ld_in.at[j], ls.at[j], lr.at[j], along_t(j))

    def send_other():
        return copy(ld_out.at[half], ld_in.at[0], ls.at[0], lr.at[0], along_t(half))

    local = [
        pltpu.make_async_copy(center, ce.at[0], own.at[0]),
        pltpu.make_async_copy(fluid, fl.at[0], own.at[1]),
        pltpu.make_async_copy(poly, pv, own.at[2]),
    ]
    for c in local:
        c.start()
    barrier = pltpu.get_barrier_semaphore()
    for p in range(1, half + 1):
        pl.semaphore_signal(barrier, inc=1, device_id=along_t(p), device_id_type=MESH)
    for m in range(1, S):
        pl.semaphore_signal(barrier, inc=1, device_id=along_s(m), device_id_type=MESH)
    fc[...] = jnp.zeros(fc.shape, jnp.bfloat16)
    fa[...] = jnp.zeros(fa.shape, jnp.float32)
    for c in local:
        c.wait()
    pl.semaphore_wait(barrier, S - 1 + half)
    for p in [half] + list(range(1, half)):
        send_center(p).start()
    for m in [1] + list(range(S - 1, 1, -1)):
        send_fluid(m).start()

    def ready_center(r):
        for g, x in enumerate(center_rows(ce[r, 0:8, :])):
            fa[0, 8 * g : 8 * g + 8, 0:wc] = x
        depth = 8 * 9
        fc[r, 0 : depth + 8, :] = fa[0, 0 : depth + 8, 0:wc].astype(jnp.bfloat16)
        high, low = split(ce[r, 3:, :] * TOP)
        chl[r, 0:nvals] = high
        chl[r, nvals:] = low

    def ready_fluid(m):
        for g, x in enumerate(fluid_rows(fl[m, 0:8, :])):
            fa[1, 8 * g : 8 * g + 8, 0:wf] = x
        ff[m] = jnp.transpose(fa[1, :, 0:wf]).astype(jnp.bfloat16)
        high, low = split(fl[m, 3:, :] * TOP)
        fhl[m, 0:nvals] = high
        fhl[m, nvals:] = low

    def squares(tile, slot):
        m, r = tile
        sq[slot] = dot(ff[m], fc[r], ((1,), (0,)))

    def values(slot):
        step = 32 if wf % 32 == 0 else wf
        for j in range(0, wf, step):
            at = pl.ds(j, step)
            s = sq[slot, at, :]
            inv = lax.rsqrt(s)
            turns = s * inv
            f = turns - jnp.round(turns)
            size = jnp.abs(f)
            rest = 0.5 - size
            q = size * rest
            value = (f * rest * inv) * ((q + MID) * q + LOW)
            high, low = split(value)
            kh[slot, at, :] = high
            kl[slot, at, :] = low

    seen = set()

    def add(ref, i, name, x):
        if (name, i) in seen:
            ref[i] += x
        else:
            ref[i] = x
            seen.add((name, i))

    def sums(tile, slot):
        m, r = tile
        k_high, k_low = kh[slot], kl[slot]
        across = ((1,), (0,))
        wide = dot(fhl[m], k_high, across)
        add(ld_out, r, "l", wide[:nvals] + wide[nvals:] + dot(fhl[m, 0:nvals], k_low, across))
        back = ((1,), (1,))
        wide = dot(chl[r], k_high, back)
        add(mo_out, m, "m", wide[:nvals] + wide[nvals:] + dot(chl[r, 0:nvals], k_low, back))

    order = tiles_of(S, T)
    pairs = [order[i : i + 2] for i in range(0, len(order), 2)]
    have_f, have_c, handed = {0}, {0}, {0}
    left_m = {m: T for m in range(S)}
    left_r = {r: S for r in range(T)}
    waiting, sent_at = [], {}
    ready_fluid(0)
    ready_center(0)

    def receive(r):
        if r <= half and r not in handed:
            send_center(r).wait_recv()
            if r < half:
                hand_on(r).start()
            handed.add(r)

    def fetch(pair):
        fresh = []
        for m, r in pair:
            if r not in have_c:
                if r <= half:
                    receive(r)
                else:
                    receive(min(r - half + 1, half - 1))
                    hand_on(r - half).wait_recv()
                fresh.append((ready_center, r))
                have_c.add(r)
            if m not in have_f:
                send_fluid(m).wait_recv()
                fresh.append((ready_fluid, m))
                have_f.add(m)
        return fresh

    def finish(j):
        send_pre(half + j).wait_recv()
        ld_out[j] += pre[j]
        send_loads(j).start()

    def done(pair, k):
        for m, r in pair:
            left_m[m] -= 1
            left_r[r] -= 1
            if m and not left_m[m]:
                send_motion(m).start()
            if r and not left_r[r]:
                if r > half:
                    send_pre(r).start()
                    sent_at[r] = k
                elif r == half:
                    send_other().start()
                else:
                    waiting.append(r)

    slot_of = lambda k, i: (k % 2) * 2 + i
    for f, i in fetch(pairs[0]):
        f(i)
    for i in range(2):
        squares(pairs[0][i], slot_of(0, i))
    for i in range(2):
        values(slot_of(0, i))
    n = len(pairs)
    for k in range(n + 1):
        fresh = fetch(pairs[k + 1]) if k + 1 < n else []
        for i in range(2):
            if k > 1:
                sums(pairs[k - 1][i], slot_of(k - 1, i))
            if k == 0:
                sums(pairs[0][i], slot_of(0, i))
        for f, i in fresh:
            f(i)
        for i in range(2):
            if k + 1 < n:
                squares(pairs[k + 1][i], slot_of(k + 1, i))
        for i in range(2):
            if 0 < k < n:
                values(slot_of(k, i))
        if k > 0:
            done(pairs[k - 1], k)
            for j in list(waiting):
                if k >= sent_at.get(half + j, n) + 3 or k == n:
                    finish(j)
                    waiting.remove(j)

    total = mo_out[0]
    affine = jnp.transpose(pv[...])
    for a in range(3):
        total = total + affine[:, a + 1 : a + 2] * fl[0, a : a + 1, :]
    total = total + affine[:, 0:1]
    order_s = list(range(S - 1, 0, -1))
    for m in order_s:
        send_motion(m).wait_recv()
        total = total + mo_in[m]
    motion[...] = total
    total = ld_out[0]
    send_other().wait_recv()
    total = total + ld_in[0]
    for j in range(half - 1, 0, -1):
        send_loads(j).wait_recv()
        total = total + ld_in[j]
    loads[...] = total
    for m in order_s:
        send_fluid(m).wait_send()
        send_motion(m).wait_send()
    for p in range(1, half + 1):
        send_center(p).wait_send()
    for p in range(1, half):
        hand_on(p).wait_send()
        send_pre(p + half).wait_send()
        send_loads(p).wait_send()
    send_other().wait_send()


def per_device(rows, cols, side, fluid_data, center_data, poly_coef):
    f32, bf16 = jnp.float32, jnp.bfloat16
    S, T = cols // side, rows * side
    height, wf = fluid_data.shape
    wc = center_data.shape[1]
    n = height - 3
    vmem = pl.BlockSpec(memory_space=pltpu.VMEM)
    hbm = pl.BlockSpec(memory_space=pltpu.HBM)
    sems = [pltpu.SemaphoreType.DMA((k,)) for k in (3, S, S, T, T, S, S, T // 2, T // 2, T // 2, T // 2)]
    return pl.pallas_call(
        functools.partial(body, rows, cols, side),
        out_shape=(jax.ShapeDtypeStruct((n, wf), f32), jax.ShapeDtypeStruct((n, wc), f32)),
        in_specs=[hbm] * 3,
        out_specs=(vmem, vmem),
        scratch_shapes=[
            pltpu.VMEM((S, height, wf), f32),
            pltpu.VMEM((T, height, wc), f32),
            pltpu.VMEM((4, n), f32),
            pltpu.VMEM((2, DEPTH, max(wf, wc)), f32),
            pltpu.VMEM((S, wf, DEPTH), bf16),
            pltpu.VMEM((T, DEPTH, wc), bf16),
            pltpu.VMEM((T, 2 * n, wc), bf16),
            pltpu.VMEM((S, 2 * n, wf), bf16),
            pltpu.VMEM((4, wf, wc), f32),
            pltpu.VMEM((4, wf, wc), bf16),
            pltpu.VMEM((4, wf, wc), bf16),
            pltpu.VMEM((S, n, wf), f32),
            pltpu.VMEM((S, n, wf), f32),
            pltpu.VMEM((T, n, wc), f32),
            pltpu.VMEM((T // 2, n, wc), f32),
            pltpu.VMEM((T // 2, n, wc), f32),
            *sems,
        ],
        compiler_params=pltpu.CompilerParams(
            collective_id=0, has_side_effects=True, vmem_limit_bytes=67_043_328
        ),
    )(fluid_data, center_data, poly_coef.T)


def solution(mesh):
    rows, cols = mesh.shape["row"], mesh.shape["col"]
    side = 2 if cols % 2 == 0 else 1
    placed = (P(None, ("row", "col")), P(None, ("col", "row")), P())
    return jax.shard_map(
        functools.partial(per_device, rows, cols, side),
        mesh=mesh,
        in_specs=placed,
        out_specs=(P(None, ("row", "col")), P(None, ("col", "row"))),
        check_vma=False,
    )
```

time: 29.1 us -> 25.7 us (0.88)
  Pallas kernels: 26.2 us -> 22.7 us
    pallas_call x1, Pallas kernels: 26.2 us -> 22.7 us  [per_device(): pl.pallas_call(functools.partial(body, rows, cols, side), out_shape=(jax....]
where the time goes in v1:
time: 25.7 us; the launch traced here: 25.4 us
  Pallas kernels  22.7 us (88%)
  local copies, waits for them, and re-layouts  2.06 us (8%)
  between operations  0.65 us (3%)
    pallas_call x1, Pallas kernels, per_device(): pl.pallas_call(functools.partial(body, rows, cols, side), out_shape=(jax....  22.7 us
    unnamed x4, local copies, waits for them, and re-layouts  2.06 us

profile of v1, /device:TPU:0, one launch (start us, length us, event | category | flops | bytes accessed | tf_op | source)
XLA Modules:
  0.0 25.4 jit_solution(2814936142343202858)
XLA Ops:
  0.6 22.7 %shard_map.50 = (f32[48,256]{1,0:T(8,128)}, f32[48,256]{1,0:T(8,128)}) custom-call(f32[51,256]{1,0:T(8,128)} %fluid.1, f32[51,256]{1,0:T(8,128)} %center.1, f32[4,48]{1,0:T(4,128)} %bitcast.1), custom_call_target="tpu_custom_call" | custom-call | tf_op jit(solution)/shard_map/pallas_call | solution.py:366
  23.4 0.0 copy-start
  23.4 1.4 %copy.7 = f32[48,256]{1,0:T(8,128)} copy(f32[48,256]{1,0:T(8,128)} %get-tuple-element.4) | data formatting | bytes 98304
  24.8 0.0 copy-done
  24.8 0.6 %copy.8 = f32[48,256]{1,0:T(8,128)} copy(f32[48,256]{1,0:T(8,128)S(1)} %copy-done) | data formatting | bytes 98304
Async XLA Ops:
  23.4 1.4 %copy-start = (f32[48,256]{1,0:T(8,128)S(1)}, f32[48,256]{1,0:T(8,128)}, u32[]{:S(2)}) copy-start(f32[48,256]{1,0:T(8,128)} %get-tuple-element.5) | copy-start | bytes 147460

commit v2 on v1

--- a/solution.py
+++ b/solution.py
@@ -99,24 +99,37 @@
     ]
 
 
-def tiles_of(S, T):
+def plan_of(S, T):
     half = T // 2
     near = list(range(1, min(half, 3)))
-    order = [(0, 0), (0, half)]
-    order += [(0, p) for p in near] + [(1, p) for p in near]
-    for p in near:
-        order += [(0, half + p), (1, half + p)]
-    for p in range(3, half):
-        order += [(0, p), (1, p), (0, half + p), (1, half + p)]
-    for m in range(S - 1, 2, -1):
-        order += [(m, r) for r in [0, half] + list(range(1, half)) + list(range(half + 1, T))]
-    order += [(2, r) for r in list(range(T - 1, half, -1)) + list(range(half - 1, 0, -1)) + [half, 0]]
-    order += [(1, 0), (1, half)]
+    far = list(range(3, half))
+    groups = [([("c", half)], [(0, 0), (0, half)])]
+    first = [(0, p) for p in near] + [(1, p) for p in near]
+    groups.append(([("c", p) for p in near] + [("f", 1)], first))
+    more = [("c", p) for p in far[:1]] + [("c", half + p) for p in near]
+    tiles = [(m, half + p) for p in near for m in (0, 1)]
+    tiles += [(m, p) for p in far[:1] for m in (0, 1)]
+    groups.append((more, tiles))
+    for p in far[1:]:
+        groups.append(([("c", p), ("c", half + p - 1)], [(0, p), (1, p), (0, half + p - 1), (1, half + p - 1)]))
+    last = far[-1:]
+    every = [0, half] + list(range(1, half)) + list(range(half + 1, T))
+    tiles = [(m, half + p) for p in last for m in (0, 1)] + [(2, r) for r in every]
+    groups.append(([("c", half + p) for p in last] + [("f", 2)], tiles))
+    for m in range(S - 2, 2, -1):
+        groups.append(([("f", m)], [(m, r) for r in every]))
+    tiles = [(S - 1, r) for r in list(range(T - 1, half, -1)) + list(range(half - 1, 0, -1)) + [half, 0]]
+    tiles += [(1, 0), (1, half)]
+    groups.append(([("f", S - 1)], tiles))
+    order, needs = [], {}
+    for need, tiles in groups:
+        needs[len(order) // 2] = need
+        order += tiles
     assert len(set(order)) == S * T == len(order)
-    return order
-
-
-def body(rows, cols, side, fluid, center, poly, motion, loads, *scratch):
+    return [order[i : i + 2] for i in range(0, len(order), 2)], needs
+
+
+def body(rows, cols, side, fluid, center, poly, out, *scratch):
     (fl, ce, pv, fa, ff, fc, chl, fhl, sq, kh, kl, mo_out, mo_in, ld_out, ld_in, pre) = scratch[:16]
     own, fs, fr, cs, cr, ms, mr, ls, lr, ps, pr = scratch[16:]
     S, T = cols // side, rows * side
@@ -183,7 +196,7 @@
     pl.semaphore_wait(barrier, S - 1 + half)
     for p in [half] + list(range(1, half)):
         send_center(p).start()
-    for m in [1] + list(range(S - 1, 1, -1)):
+    for m in [1] + list(range(2, S)):
         send_fluid(m).start()
 
     def ready_center(r):
@@ -242,9 +255,8 @@
         wide = dot(chl[r], k_high, back)
         add(mo_out, m, "m", wide[:nvals] + wide[nvals:] + dot(chl[r, 0:nvals], k_low, back))
 
-    order = tiles_of(S, T)
-    pairs = [order[i : i + 2] for i in range(0, len(order), 2)]
-    have_f, have_c, handed = {0}, {0}, {0}
+    pairs, needs = plan_of(S, T)
+    handed = {0}
     left_m = {m: T for m in range(S)}
     left_r = {r: S for r in range(T)}
     waiting, sent_at = [], {}
@@ -258,21 +270,18 @@
                 hand_on(r).start()
             handed.add(r)
 
-    def fetch(pair):
+    def fetch(k):
         fresh = []
-        for m, r in pair:
-            if r not in have_c:
-                if r <= half:
-                    receive(r)
+        for kind, i in needs.get(k, []):
+            if kind == "f":
+                send_fluid(i).wait_recv()
+                fresh.append((ready_fluid, i))
+            else:
+                if i <= half:
+                    receive(i)
                 else:
-                    receive(min(r - half + 1, half - 1))
-                    hand_on(r - half).wait_recv()
-                fresh.append((ready_center, r))
-                have_c.add(r)
-            if m not in have_f:
-                send_fluid(m).wait_recv()
-                fresh.append((ready_fluid, m))
-                have_f.add(m)
+                    hand_on(i - half).wait_recv()
+                fresh.append((ready_center, i))
         return fresh
 
     def finish(j):
@@ -296,7 +305,7 @@
                     waiting.append(r)
 
     slot_of = lambda k, i: (k % 2) * 2 + i
-    for f, i in fetch(pairs[0]):
+    for f, i in fetch(0):
         f(i)
     for i in range(2):
         squares(pairs[0][i], slot_of(0, i))
@@ -304,7 +313,7 @@
         values(slot_of(0, i))
     n = len(pairs)
     for k in range(n + 1):
-        fresh = fetch(pairs[k + 1]) if k + 1 < n else []
+        fresh = fetch(k + 1) if k + 1 < n else []
         for i in range(2):
             if k > 1:
                 sums(pairs[k - 1][i], slot_of(k - 1, i))
@@ -321,7 +330,7 @@
         if k > 0:
             done(pairs[k - 1], k)
             for j in list(waiting):
-                if k >= sent_at.get(half + j, n) + 3 or k == n:
+                if k >= sent_at.get(half + j, n) + 2 or k == n:
                     finish(j)
                     waiting.remove(j)
 
@@ -334,14 +343,14 @@
     for m in order_s:
         send_motion(m).wait_recv()
         total = total + mo_in[m]
-    motion[...] = total
+    out[0, :, 0:wf] = total
     total = ld_out[0]
     send_other().wait_recv()
     total = total + ld_in[0]
     for j in range(half - 1, 0, -1):
         send_loads(j).wait_recv()
         total = total + ld_in[j]
-    loads[...] = total
+    out[1, :, 0:wc] = total
     for m in order_s:
         send_fluid(m).wait_send()
         send_motion(m).wait_send()
@@ -363,11 +372,11 @@
     vmem = pl.BlockSpec(memory_space=pltpu.VMEM)
     hbm = pl.BlockSpec(memory_space=pltpu.HBM)
     sems = [pltpu.SemaphoreType.DMA((k,)) for k in (3, S, S, T, T, S, S, T // 2, T // 2, T // 2, T // 2)]
-    return pl.pallas_call(
+    both = pl.pallas_call(
         functools.partial(body, rows, cols, side),
-        out_shape=(jax.ShapeDtypeStruct((n, wf), f32), jax.ShapeDtypeStruct((n, wc), f32)),
+        out_shape=jax.ShapeDtypeStruct((2, n, max(wf, wc)), f32),
         in_specs=[hbm] * 3,
-        out_specs=(vmem, vmem),
+        out_specs=vmem,
         scratch_shapes=[
             pltpu.VMEM((S, height, wf), f32),
             pltpu.VMEM((T, height, wc), f32),
@@ -391,6 +400,7 @@
             collective_id=0, has_side_effects=True, vmem_limit_bytes=67_043_328
         ),
     )(fluid_data, center_data, poly_coef.T)
+    return both[0, :, :wf], both[1, :, :wc]
 
 
 def solution(mesh):

time: 25.7 us -> 24.7 us (0.961)
  local copies, waits for them, and re-layouts: 2.06 us -> 1.46 us
  Pallas kernels: 22.7 us -> 22.4 us
    unnamed x4 -> x0, local copies, waits for them, and re-layouts: 2.06 us -> none
    squeeze x0 -> x1, local copies, waits for them, and re-layouts: none -> 1.46 us  [per_device(): return (both[0, :, :wf], both[1, :, :wc])]
    pallas_call x1, Pallas kernels: 22.7 us -> 22.4 us  [per_device(): pl.pallas_call(functools.partial(body, rows, cols, side), out_shape=jax.S...]
where the time goes in v2:
time: 24.7 us; the launch traced here: 24.5 us
  Pallas kernels  22.4 us (91%)
  local copies, waits for them, and re-layouts  1.46 us (6%)
  between operations  0.64 us (3%)
    pallas_call x1, Pallas kernels, per_device(): pl.pallas_call(functools.partial(body, rows, cols, side), out_shape=jax.S...  22.4 us
    squeeze x1, local copies, waits for them, and re-layouts, per_device(): return (both[0, :, :wf], both[1, :, :wc])  1.46 us

profile of v2, /device:TPU:0, one launch (start us, length us, event | category | flops | bytes accessed | tf_op | source)
XLA Modules:
  0.0 24.5 jit_solution(14894300416840509468)
XLA Ops:
  0.6 22.4 %shard_map.50 = f32[2,48,256]{2,1,0:T(8,128)} custom-call(f32[51,256]{1,0:T(8,128)} %fluid.1, f32[51,256]{1,0:T(8,128)} %center.1, f32[4,48]{1,0:T(4,128)} %bitcast.5), custom_call_target="tpu_custom_call" | custom-call | tf_op jit(solution)/shard_map/pallas_call | solution.py:375
  23.0 1.5 %slice_bitcast_fusion = (f32[48,256]{1,0:T(8,128)}, f32[48,256]{1,0:T(8,128)}) fusion(f32[2,48,256]{2,1,0:T(8,128)} %shard_map.50), kind=kLoop, calls=%fused_computation | loop fusion | bytes 196608 | tf_op jit(solution)/shard_map/squeeze | solution.py:403

commit v3 on v2

--- a/solution.py
+++ b/solution.py
@@ -104,7 +104,7 @@
     near = list(range(1, min(half, 3)))
     far = list(range(3, half))
     groups = [([("c", half)], [(0, 0), (0, half)])]
-    first = [(0, p) for p in near] + [(1, p) for p in near]
+    first = [(0, p) for p in near] + [(1, 0), (1, half)]
     groups.append(([("c", p) for p in near] + [("f", 1)], first))
     more = [("c", p) for p in far[:1]] + [("c", half + p) for p in near]
     tiles = [(m, half + p) for p in near for m in (0, 1)]
@@ -119,7 +119,7 @@
     for m in range(S - 2, 2, -1):
         groups.append(([("f", m)], [(m, r) for r in every]))
     tiles = [(S - 1, r) for r in list(range(T - 1, half, -1)) + list(range(half - 1, 0, -1)) + [half, 0]]
-    tiles += [(1, 0), (1, half)]
+    tiles += [(1, p) for p in near]
     groups.append(([("f", S - 1)], tiles))
     order, needs = [], {}
     for need, tiles in groups:

time: 24.7 us -> 24.2 us (0.980)
  Pallas kernels: 22.4 us -> 21.9 us
    pallas_call x1, Pallas kernels: 22.4 us -> 21.9 us  [per_device(): pl.pallas_call(functools.partial(body, rows, cols, side), out_shape=jax.S...]
where the time goes in v3:
time: 24.2 us; the launch traced here: 24 us
  Pallas kernels  21.9 us (90%)
  local copies, waits for them, and re-layouts  1.46 us (6%)
  between operations  0.64 us (3%)
    pallas_call x1, Pallas kernels, per_device(): pl.pallas_call(functools.partial(body, rows, cols, side), out_shape=jax.S...  21.9 us
    squeeze x1, local copies, waits for them, and re-layouts, per_device(): return (both[0, :, :wf], both[1, :, :wc])  1.46 us

profile of v3, /device:TPU:0, one launch (start us, length us, event | category | flops | bytes accessed | tf_op | source)
XLA Modules:
  0.0 24.0 jit_solution(9882528906418867838)
XLA Ops:
  0.6 21.9 %shard_map.50 = f32[2,48,256]{2,1,0:T(8,128)} custom-call(f32[51,256]{1,0:T(8,128)} %fluid.1, f32[51,256]{1,0:T(8,128)} %center.1, f32[4,48]{1,0:T(4,128)} %bitcast.5), custom_call_target="tpu_custom_call" | custom-call | tf_op jit(solution)/shard_map/pallas_call | solution.py:375
  22.5 1.5 %slice_bitcast_fusion = (f32[48,256]{1,0:T(8,128)}, f32[48,256]{1,0:T(8,128)}) fusion(f32[2,48,256]{2,1,0:T(8,128)} %shard_map.50), kind=kLoop, calls=%fused_computation | loop fusion | bytes 196608 | tf_op jit(solution)/shard_map/squeeze | solution.py:403

commit v4 on v3

--- a/solution.py
+++ b/solution.py
@@ -311,14 +311,14 @@
         squares(pairs[0][i], slot_of(0, i))
     for i in range(2):
         values(slot_of(0, i))
+    for i in range(2):
+        sums(pairs[0][i], slot_of(0, i))
     n = len(pairs)
     for k in range(n + 1):
         fresh = fetch(k + 1) if k + 1 < n else []
         for i in range(2):
             if k > 1:
                 sums(pairs[k - 1][i], slot_of(k - 1, i))
-            if k == 0:
-                sums(pairs[0][i], slot_of(0, i))
         for f, i in fresh:
             f(i)
         for i in range(2):

time: 24.2 us -> 24.2 us (level)
  no operation moved by 1% of the time
where the time goes in v4:
time: 24.2 us; the launch traced here: 23.9 us
  Pallas kernels  21.8 us (90%)
  local copies, waits for them, and re-layouts  1.46 us (6%)
  between operations  0.64 us (3%)
    pallas_call x1, Pallas kernels, per_device(): pl.pallas_call(functools.partial(body, rows, cols, side), out_shape=jax.S...  21.8 us
    squeeze x1, local copies, waits for them, and re-layouts, per_device(): return (both[0, :, :wf], both[1, :, :wc])  1.46 us

profile of v4, /device:TPU:0, one launch (start us, length us, event | category | flops | bytes accessed | tf_op | source)
XLA Modules:
  0.0 23.9 jit_solution(17770376149473925184)
XLA Ops:
  0.6 21.8 %shard_map.50 = f32[2,48,256]{2,1,0:T(8,128)} custom-call(f32[51,256]{1,0:T(8,128)} %fluid.1, f32[51,256]{1,0:T(8,128)} %center.1, f32[4,48]{1,0:T(4,128)} %bitcast.5), custom_call_target="tpu_custom_call" | custom-call | tf_op jit(solution)/shard_map/pallas_call | solution.py:375
  22.5 1.5 %slice_bitcast_fusion = (f32[48,256]{1,0:T(8,128)}, f32[48,256]{1,0:T(8,128)}) fusion(f32[2,48,256]{2,1,0:T(8,128)} %shard_map.50), kind=kLoop, calls=%fused_computation | loop fusion | bytes 196608 | tf_op jit(solution)/shard_map/squeeze | solution.py:403

commit v5 on v4

--- a/solution.py
+++ b/solution.py
@@ -204,6 +204,8 @@
             fa[0, 8 * g : 8 * g + 8, 0:wc] = x
         depth = 8 * 9
         fc[r, 0 : depth + 8, :] = fa[0, 0 : depth + 8, 0:wc].astype(jnp.bfloat16)
+
+    def values_center(r):
         high, low = split(ce[r, 3:, :] * TOP)
         chl[r, 0:nvals] = high
         chl[r, nvals:] = low
@@ -212,6 +214,8 @@
         for g, x in enumerate(fluid_rows(fl[m, 0:8, :])):
             fa[1, 8 * g : 8 * g + 8, 0:wf] = x
         ff[m] = jnp.transpose(fa[1, :, 0:wf]).astype(jnp.bfloat16)
+
+    def values_fluid(m):
         high, low = split(fl[m, 3:, :] * TOP)
         fhl[m, 0:nvals] = high
         fhl[m, nvals:] = low
@@ -262,6 +266,8 @@
     waiting, sent_at = [], {}
     ready_fluid(0)
     ready_center(0)
+    values_fluid(0)
+    values_center(0)
 
     def receive(r):
         if r <= half and r not in handed:
@@ -307,6 +313,7 @@
     slot_of = lambda k, i: (k % 2) * 2 + i
     for f, i in fetch(0):
         f(i)
+        values_center(i)
     for i in range(2):
         squares(pairs[0][i], slot_of(0, i))
     for i in range(2):
@@ -324,6 +331,8 @@
         for i in range(2):
             if k + 1 < n:
                 squares(pairs[k + 1][i], slot_of(k + 1, i))
+        for f, i in fresh:
+            (values_center if f is ready_center else values_fluid)(i)
         for i in range(2):
             if 0 < k < n:
                 values(slot_of(k, i))

time: 24.2 us -> 24.2 us (level)
  no operation moved by 1% of the time
where the time goes in v5:
time: 24.2 us; the launch traced here: 23.9 us
  Pallas kernels  21.8 us (90%)
  local copies, waits for them, and re-layouts  1.46 us (6%)
  between operations  0.64 us (3%)
    pallas_call x1, Pallas kernels, per_device(): pl.pallas_call(functools.partial(body, rows, cols, side), out_shape=jax.S...  21.8 us
    squeeze x1, local copies, waits for them, and re-layouts, per_device(): return (both[0, :, :wf], both[1, :, :wc])  1.46 us

profile of v5, /device:TPU:0, one launch (start us, length us, event | category | flops | bytes accessed | tf_op | source)
XLA Modules:
  0.0 23.9 jit_solution(17770376149473925184)
XLA Ops:
  0.6 21.8 %shard_map.50 = f32[2,48,256]{2,1,0:T(8,128)} custom-call(f32[51,256]{1,0:T(8,128)} %fluid.1, f32[51,256]{1,0:T(8,128)} %center.1, f32[4,48]{1,0:T(4,128)} %bitcast.5), custom_call_target="tpu_custom_call" | custom-call | tf_op jit(solution)/shard_map/pallas_call | solution.py:384
  22.5 1.5 %slice_bitcast_fusion = (f32[48,256]{1,0:T(8,128)}, f32[48,256]{1,0:T(8,128)}) fusion(f32[2,48,256]{2,1,0:T(8,128)} %shard_map.50), kind=kLoop, calls=%fused_computation | loop fusion | bytes 196608 | tf_op jit(solution)/shard_map/squeeze | solution.py:412
